TPU v7x, 32 devices: a whole 2x2x4 slice. The times are simulated.
32 devices in a mesh: dp: 32 (over z, y, x, core), mp: 1.
Axes of the slice: x: 2, y: 2, z: 4, core: 2. Of those that a mesh axis runs over, the one named last changes fastest.
Arguments:
- gradients: bfloat16 [32, 512, 6144], P('dp', None, 'mp'), may hold values from -48 to 48
- weights: bfloat16 [512, 6144], P(None, 'mp'), may hold values from -3 to 3
- master: float32 [512, 6144], P('dp', 'mp'), may hold values from -6 to 6
- moment_one: float32 [512, 6144], P('dp', 'mp'), may hold values from -6 to 6
- moment_two: float32 [512, 6144], P('dp', 'mp'), may hold values from 0.25 to 4
- group_ids: int32 [512], replicated, may hold values from 0 to 15, never falling along the last dimension, each value on 1 to 64 neighbouring positions
Outputs:
- new_weights: bfloat16 [512, 6144], P(None, 'mp')
- new_master: float32 [512, 6144], P('dp', 'mp')
- new_first: float32 [512, 6144], P('dp', 'mp')
- new_second: float32 [512, 6144], P('dp', 'mp')
Inputs may be any that keep to these rules, and one draw needn't show every extreme that they name: `group_ids`: group numbers never fall along the rows; each group has 1 to 64 rows and every group is present.
All inputs are finite; a program needn't handle non-finite values.
Results may differ from a plain program's by a relative error of at most 0.001.
The roundings to bfloat16 on the way count: a program that leaves them out, or rounds other values in their place, can miss the bound.
Values may be sent and summed in bfloat16 or wider, within the bound.
No kernel may reach another device: no remote copies, remote signals or barrier semaphores. Data moves between devices by JAX's collectives and lax.ppermute only.
A program may use at most 64 MiB of HBM per device.

v0:
```python
import jax
import jax.numpy as jnp
from jax import lax
from jax.sharding import PartitionSpec as P

beta_one = 0.9
beta_two = 0.999
adam_eps = 1e-06
weight_decay = 0.01
learn_rate = 0.04
step_count = 100


def on_device(gradients, weights, master, moment_one, moment_two, group_ids):
    owned_rows = master.shape[0]
    rows_all = weights.shape[0]
    groups = rows_all // 32
    replicas = lax.axis_size("dp")
    my_index = lax.axis_index("dp")
    first_own = my_index * owned_rows
    my_groups = lax.dynamic_slice_in_dim(group_ids, first_own, owned_rows, 0)
    member = (my_groups[:, None] == jnp.arange(groups, dtype=jnp.int32)[None, :]).astype(
        jnp.float32
    )
    weight_rows = jnp.dot(jnp.sum(master * master, axis=1), member, precision=lax.Precision.HIGHEST)
    local_grad = gradients[0]
    summed = lax.psum_scatter(local_grad.astype(jnp.float32), "dp", scatter_dimension=0, tiled=True)
    grad_mean = summed / replicas
    new_first = beta_one * moment_one + (1.0 - beta_one) * grad_mean
    new_second = beta_two * moment_two + (1.0 - beta_two) * grad_mean * grad_mean
    correct_one = 1.0 - beta_one**step_count
    correct_two = 1.0 - beta_two**step_count
    update = (
        new_first / correct_one / (jnp.sqrt(new_second / correct_two) + adam_eps)
        + weight_decay * master
    )
    update_rows = jnp.dot(jnp.sum(update * update, axis=1), member, precision=lax.Precision.HIGHEST)
    weight_sq, update_sq = lax.psum((weight_rows, update_rows), ("dp", "mp"))
    trust_ratio = jnp.sqrt(weight_sq / (update_sq + 1e-06))
    row_ratio = jnp.dot(member, trust_ratio, precision=lax.Precision.HIGHEST)
    step_size = learn_rate * row_ratio[:, None] * update
    new_master = master - step_size
    delta_bf = (-step_size).astype(jnp.bfloat16)
    new_weights = (
        weights.astype(jnp.float32)
        + lax.all_gather(delta_bf, "dp", axis=0, tiled=True).astype(jnp.float32)
    ).astype(jnp.bfloat16)
    return (new_weights, new_master, new_first, new_second)


def solution(mesh):
    placed = (P("dp", None, "mp"), P(None, "mp"), P("dp", "mp"), P("dp", "mp"), P("dp", "mp"), P())
    return jax.shard_map(
        on_device,
        mesh=mesh,
        in_specs=placed,
        out_specs=(P(None, "mp"), P("dp", "mp"), P("dp", "mp"), P("dp", "mp")),
        check_vma=False,
    )
```

profile of v0, /device:TPU:0, one launch (start us, length us, event | category | flops | bytes accessed | tf_op | source)
XLA Modules:
  0.0 302.7 jit_solution(6108356624688245434)
XLA Ops:
  7.2 0.0 reduce-scatter.2.cloned.1.call-start
  7.2 9.0 %bitcast_convert_fusion = f32[512,6144]{1,0:T(8,128)} fusion(bf16[1,512,6144]{2,1,0:T(8,128)(2,1)} %param.6), kind=kLoop, calls=%fused_computation.1 | loop fusion | flops 3145728 | bytes 18874368 | tf_op jit(solution)/shard_map/convert_element_type | solution.py:27
  16.2 0.0 copy-start
  16.2 0.0 copy-start.1
  16.2 0.0 copy-start.2
  16.2 0.0 reduce-scatter.2.cloned.1.call-update
  16.2 0.0 all-gather.2.cloned.1.call-start
  16.3 0.8 dynamic_slice.3
  17.1 156.8 %reduce-scatter.2.cloned.1.call-done = f32[16,6144]{1,0:T(8,128)} async-done(((f32[512,6144]{1,0:T(8,128)}), f32[16,6144]{1,0:T(8,128)}) %reduce-scatter.2.cloned.1.call-update) | async-done | bytes 393232 | tf_op jit(solution)/shard_map/reduce_scatter | solution.py:27
  174.0 0.0 copy-done
  174.0 0.0 copy-done.1
  174.0 0.0 copy-done.2
  174.0 2.3 multiply_reduce_fusion
  176.3 0.2 convolution_bitcast_fusion.1
  176.5 0.2 convolution_bitcast_fusion.2
  176.7 39.4 %all-reduce = (f32[16]{0:T(128)S(1)}, f32[16]{0:T(128)S(1)}) all-reduce(f32[16]{0:T(128)S(1)} %convolution_bitcast_fusion.2, f32[16]{0:T(128)S(1)} %convolution_bitcast_fusion.1), channel_id=1, replica_groups=mesh['dp'=32,'mp'=1] {'dp','mp'}, use_global_device_ids=true, to_apply=%region_1.0 | all-reduce | flops 32 | bytes 256 | tf_op jit(solution)/shard_map/psum | solution.py:38
  216.0 0.2 fusion
  216.2 0.9 multiply_subtract_fusion
  217.2 0.0 all-gather.2.cloned.1.call-update
  217.2 68.7 %all-gather.2.cloned.1.call-done = bf16[512,6144]{1,0:T(8,128)(2,1)} async-done(((bf16[16,6144]{1,0:T(8,128)(2,1)}), bf16[512,6144]{1,0:T(8,128)(2,1)}) %all-gather.2.cloned.1.call-update) | async-done | bytes 6291472 | tf_op jit(solution)/shard_map/all_gather | solution.py:46
  285.9 10.0 %add_convert_fusion = bf16[512,6144]{1,0:T(8,128)(2,1)} fusion(bf16[512,6144]{1,0:T(8,128)(2,1)} %all-gather.2.cloned.1.call-done, bf16[512,6144]{1,0:T(8,128)(2,1)} %param.7), kind=kLoop, calls=%fused_computation | loop fusion | flops 12582912 | bytes 18874368 | tf_op jit(solution)/shard_map/convert_element_type | solution.py:47
Async XLA Ops:
  7.2 166.8 %reduce-scatter.2.cloned.1.call-start = ((), (), s32[]{:S(2)}) async-start(), calls=%async_computation.1 | async-start | bytes 12976128 | tf_op jit(solution)/shard_map/reduce_scatter | solution.py:27
  16.2 157.8 %copy-start = (f32[16,6144]{1,0:T(8,128)S(1)}, f32[16,6144]{1,0:T(8,128)}, u32[]{:S(2)}) copy-start(f32[16,6144]{1,0:T(8,128)} %param.8) | copy-start | bytes 1179652
  16.2 157.8 %copy-start.1 = (f32[16,6144]{1,0:T(8,128)S(1)}, f32[16,6144]{1,0:T(8,128)}, u32[]{:S(2)}) copy-start(f32[16,6144]{1,0:T(8,128)} %param.9) | copy-start | bytes 1179652
  16.2 157.8 %copy-start.2 = (f32[16,6144]{1,0:T(8,128)S(1)}, f32[16,6144]{1,0:T(8,128)}, u32[]{:S(2)}) copy-start(f32[16,6144]{1,0:T(8,128)} %param.10) | copy-start | bytes 1179652
  16.2 269.7 %all-gather.2.cloned.1.call-start = ((), (), s32[]{:S(2)}) async-start(), calls=%async_computation.2 | async-start | bytes 6488064 | tf_op jit(solution)/shard_map/all_gather | solution.py:46
Sparse Core Ops, SparseCore 0:
  16.4 157.5 reduce-scatter.1
  217.3 68.5 all-gather.1
where the time goes:
time: 303 us
  waiting for transfers between devices  226 us (75%)
  blocking collectives  39.4 us (13%)
  other arithmetic  22.2 us (7%)
  between operations  14 us (5%)
    reduce_scatter x1, waiting for transfers between devices, on_device(): lax.psum_scatter(local_grad.astype(jnp.float32), 'dp', scatter_dimension=...  157 us
    all_gather x1, waiting for transfers between devices, on_device(): lax.all_gather(delta_bf, 'dp', axis=0, tiled=True).astype(jnp.float32)  68.7 us
    psum x1, blocking collectives, on_device(): weight_sq, update_sq = lax.psum((weight_rows, update_rows), ('dp', 'mp'))  39.4 us
    convert_element_type x1, other arithmetic, on_device(): new_weights = (weights.astype(jnp.float32) + lax.all_gather(delta_bf, 'dp...  9.96 us
    convert_element_type x1, other arithmetic, on_device(): local_grad.astype(jnp.float32)  8.99 us
  transfers between devices with their start and end apart: 2, of which 2 were waited for; matrix products, arithmetic and copies ran while one was open for 0% of the time, Pallas kernels for 0%

commit v1 on v0

--- a/solution.py
+++ b/solution.py
@@ -43,7 +43,9 @@
     delta_bf = (-step_size).astype(jnp.bfloat16)
     new_weights = (
         weights.astype(jnp.float32)
-        + lax.all_gather(delta_bf, "dp", axis=0, tiled=True).astype(jnp.float32)
+        + jnp.concatenate(
+            lax.all_to_all(jnp.stack([delta_bf] * lax.axis_size("dp")), "dp", 0, 0), axis=0
+        ).astype(jnp.float32)
     ).astype(jnp.bfloat16)
     return (new_weights, new_master, new_first, new_second)
 

time: 303 us -> 376 us (1.24)
  blocking collectives: 39.4 us -> 182 us
  waiting for transfers between devices: 226 us -> 157 us
    all_to_all x0 -> x1, blocking collectives: none -> 142 us  [on_device(): lax.all_to_all(jnp.stack([delta_bf] * lax.axis_size('dp')), 'dp', 0, 0)]
    all_gather x1 -> x0, waiting for transfers between devices: 68.7 us -> none  [on_device(): lax.all_gather(delta_bf, 'dp', axis=0, tiled=True).astype(jnp.float32)]
  transfers between devices with their start and end apart: 2 -> 1, of which waited for: 2 -> 1; matrix products, arithmetic and copies ran while one was open for 0% -> 0% of each run, Pallas kernels for 0% -> 0%
where the time goes in v1:
time: 376 us; the launch traced here: 375 us
  blocking collectives  182 us (48%)
  waiting for transfers between devices  157 us (42%)
  other arithmetic  20.3 us (5%)
  between operations  14 us (4%)
    reduce_scatter x1, waiting for transfers between devices, on_device(): lax.psum_scatter(local_grad.astype(jnp.float32), 'dp', scatter_dimension=...  157 us
    all_to_all x1, blocking collectives, on_device(): lax.all_to_all(jnp.stack([delta_bf] * lax.axis_size('dp')), 'dp', 0, 0)  142 us
    psum x1, blocking collectives, on_device(): weight_sq, update_sq = lax.psum((weight_rows, update_rows), ('dp', 'mp'))  39.4 us
    convert_element_type x1, other arithmetic, on_device(): local_grad.astype(jnp.float32)  9 us
    convert_element_type x1, other arithmetic, on_device(): new_weights = (weights.astype(jnp.float32) + jnp.concatenate(lax.all_to_a...  8.14 us
  transfers between devices with their start and end apart: 1, of which 1 were waited for; matrix products, arithmetic and copies ran while one was open for 0% of the time, Pallas kernels for 0%

profile of v1, /device:TPU:0, one launch (start us, length us, event | category | flops | bytes accessed | tf_op | source)
XLA Modules:
  0.0 375.2 jit_solution(5715704195342332693)
XLA Ops:
  7.2 0.0 reduce-scatter.2.cloned.1.call-start
  7.2 9.0 %bitcast_convert_fusion = f32[512,6144]{1,0:T(8,128)} fusion(bf16[1,512,6144]{2,1,0:T(8,128)(2,1)} %param.6), kind=kLoop, calls=%fused_computation.2 | loop fusion | flops 3145728 | bytes 18874368 | tf_op jit(solution)/shard_map/convert_element_type | solution.py:27
  16.2 0.0 copy-start
  16.2 0.0 copy-start.1
  16.2 0.0 copy-start.2
  16.2 0.0 reduce-scatter.2.cloned.1.call-update
  16.2 0.8 dynamic_slice.3
  17.1 156.9 %reduce-scatter.2.cloned.1.call-done = f32[16,6144]{1,0:T(8,128)} async-done(((f32[512,6144]{1,0:T(8,128)}), f32[16,6144]{1,0:T(8,128)}) %reduce-scatter.2.cloned.1.call-update) | async-done | bytes 393232 | tf_op jit(solution)/shard_map/reduce_scatter | solution.py:27
  174.0 0.0 copy-done
  174.0 0.0 copy-done.1
  174.0 0.0 copy-done.2
  174.0 2.3 multiply_reduce_fusion
  176.3 0.2 convolution_bitcast_fusion.1
  176.5 0.2 convolution_bitcast_fusion.2
  176.7 39.4 %all-reduce = (f32[16]{0:T(128)S(1)}, f32[16]{0:T(128)S(1)}) all-reduce(f32[16]{0:T(128)S(1)} %convolution_bitcast_fusion.2, f32[16]{0:T(128)S(1)} %convolution_bitcast_fusion.1), channel_id=1, replica_groups=mesh['dp'=32,'mp'=1] {'dp','mp'}, use_global_device_ids=true, to_apply=%region_1.0 | all-reduce | flops 32 | bytes 256 | tf_op jit(solution)/shard_map/psum | solution.py:38
  216.1 0.2 fusion.1
  216.2 0.9 multiply_subtract_fusion
  217.1 0.7 stack.2
  217.9 142.4 %all_to_all.5 = bf16[32,16,6144]{2,1,0:T(8,128)(2,1)S(1)} all-to-all(bf16[32,16,6144]{2,1,0:T(8,128)(2,1)S(1)} %stack.2), channel_id=1, replica_groups=mesh['dp'=32,'mp'=1] {'dp'}, dimensions={0} | all-to-all | bytes 12582912 | tf_op jit(solution)/shard_map/all_to_all | solution.py:47
  360.2 8.1 %fusion = bf16[512,6144]{1,0:T(8,128)(2,1)} fusion(bf16[512,6144]{1,0:T(8,128)(2,1)} %param.7, bf16[32,16,6144]{2,1,0:T(8,128)(2,1)S(1)} %all_to_all.5), kind=kLoop, calls=%fused_computation.1 | loop fusion | flops 12582912 | bytes 18874368 | tf_op jit(solution)/shard_map/convert_element_type | solution.py:49
Async XLA Ops:
  7.2 166.8 %reduce-scatter.2.cloned.1.call-start = ((), (), s32[]{:S(2)}) async-start(), calls=%async_computation.2 | async-start | bytes 12976128 | tf_op jit(solution)/shard_map/reduce_scatter | solution.py:27
  16.2 157.8 %copy-start = (f32[16,6144]{1,0:T(8,128)S(1)}, f32[16,6144]{1,0:T(8,128)}, u32[]{:S(2)}) copy-start(f32[16,6144]{1,0:T(8,128)} %param.8) | copy-start | bytes 1179652
  16.2 157.8 %copy-start.1 = (f32[16,6144]{1,0:T(8,128)S(1)}, f32[16,6144]{1,0:T(8,128)}, u32[]{:S(2)}) copy-start(f32[16,6144]{1,0:T(8,128)} %param.9) | copy-start | bytes 1179652
  16.2 157.8 %copy-start.2 = (f32[16,6144]{1,0:T(8,128)S(1)}, f32[16,6144]{1,0:T(8,128)}, u32[]{:S(2)}) copy-start(f32[16,6144]{1,0:T(8,128)} %param.10) | copy-start | bytes 1179652
Sparse Core Ops, SparseCore 0:
  16.4 157.5 reduce-scatter.1
